TPU v7x, 32 devices: a 4x4x1 block of a 4x4x8 slice. The times are simulated.
32 devices in a mesh: rep: 1 (over z), dp: 32 (over x, y, core).
Axes of the slice: x: 4, y: 4, z: 1, core: 2. Of those that a mesh axis runs over, the one named last changes fastest.
The devices are a block of a 4x4x8 slice.
Arguments:
- a: bfloat16 [32, 2, 4096, 1536], P(('rep', 'dp'))
- g: bfloat16 [32, 2, 4096, 4224], P(('rep', 'dp'))
Outputs:
- output: bfloat16 [2, 1536, 4224], P('rep')
All inputs are finite; a program needn't handle non-finite values.
Results may differ from a plain program's by a relative error of at most 0.012.
Values are sent between devices in bfloat16 or wider.
A program may use at most 768 MiB of HBM per device.

v0:
```python
import jax
import jax.numpy as jnp


def solution(mesh):
    groups = mesh.shape["rep"]

    def step(a, g):
        a, g = (t.reshape(groups, -1, *t.shape[1:]) for t in (a, g))
        sums = jnp.einsum("rsntd,rsntf->rndf", a, g, preferred_element_type=jnp.float32)
        return sums.astype(jnp.bfloat16).reshape(-1, *sums.shape[2:])

    return step
```

profile of v0, /device:TPU:97, one launch (start us, length us, event | category | flops | bytes accessed | tf_op | source)
XLA Modules:
  0.0 478.3 jit_solution(18037932158254583779)
XLA Ops:
  0.0 128.5 %fusion = f32[2,1536,4224]{2,1,0:T(8,128)} fusion(bf16[1,2,4096,4224]{3,2,1,0:T(8,128)(2,1)} %param.1, bf16[1,2,4096,1536]{3,2,1,0:T(8,128)(2,1)} %param), kind=kOutput, calls=%fused_computation | convolution fusion | flops 106300440576 | bytes 146276352 | tf_op jit(solution)/rsntd,rsntf->rndf/dot_general | solution.py:10
  128.5 349.8 %all-reduce.2 = bf16[2,1536,4224]{2,1,0:T(8,128)(2,1)} all-reduce(f32[2,1536,4224]{2,1,0:T(8,128)} %fusion), channel_id=1, replica_groups=mesh['axis_0'=32] {'axis_0'}, use_global_device_ids=true, to_apply=%add.clone | all-reduce | flops 12976128 | bytes 77856768 | tf_op jit(solution)/rsntd,rsntf->rndf/dot_general | solution.py:10
where the time goes:
time: 478 us
  blocking collectives  350 us (73%)
  matrix products  128 us (27%)
    dot_general x1, blocking collectives, step(): jnp.einsum('rsntd,rsntf->rndf', a, g, preferred_element_type=jnp.float32)  350 us
    dot_general x1, matrix products, step(): jnp.einsum('rsntd,rsntf->rndf', a, g, preferred_element_type=jnp.float32)  128 us

commit v1 on v0

v1 whole, which is shorter than its diff:
```python
import math

import jax
import jax.numpy as jnp
from jax import lax
from jax.experimental import pallas as pl
from jax.experimental.pallas import tpu as pltpu
from jax.sharding import PartitionSpec as P

MESH = pl.DeviceIdType.MESH
LANES = 128
F32 = jnp.float32
BF16 = jnp.bfloat16
OFFSETS = (0, 2, 4, 6, 8, 10, 12, 14, 16, 18)


def _reduce_kernel(side, mats, tiles, a, g, x, abuf, gbuf, acc, sd, s1, r, s2,
                   ssem, rsem, asem, gsem, credit):
    rows = x.shape[1]
    half = rows // 2
    blk = half // side
    sub = blk // side
    chunks = mats * tiles // 2
    mixed = tiles // 2 if tiles % 2 else -1
    nacc, ns1, nr, ns2 = acc.shape[0], s1.shape[0], r.shape[0], s2.shape[0]
    nss = ssem.shape[0]

    me = lax.axis_index("dp")
    core = lax.rem(me, 2)
    cy = lax.rem(me // 2, side)
    cx = me // (2 * side)
    p = jnp.where(core == 0, cx, cy)
    q = jnp.where(core == 0, cy, cx)

    def dev(i, j):
        return jnp.where(core == 0, (i * side + j) * 2, (j * side + i) * 2 + 1)

    def wrap(v):
        return lax.rem(v + 2 * side, side)

    first = (dev(wrap(p + 1), q), dev(wrap(p - 1), q))
    second = (dev(p, wrap(q + 1)), dev(p, wrap(q - 1)))
    partner = me + 1 - 2 * core
    mine = pl.multiple_of(core * half, half)
    other = pl.multiple_of((1 - core) * half, half)

    bar = pltpu.get_barrier_semaphore()
    for d in (*first, *second, partner):
        pl.semaphore_signal(bar, 1, device_id={"dp": d}, device_id_type=MESH)

    def copy(n, kind, src, dst, to):
        return pltpu.make_async_remote_copy(
            src_ref=src, dst_ref=dst, send_sem=ssem.at[lax.rem(n, nss), kind],
            recv_sem=rsem.at[n, kind], device_id={"dp": to}, device_id_type=MESH)

    def row(i, j=0):
        return pl.multiple_of(mine + wrap(i) * blk + wrap(j) * sub, sub)

    def pair(n, start, size):
        return x.at[pl.ds(2 * n, 2), pl.ds(start, size), :]

    def one(n, h, start, size):
        return x.at[2 * n + h, pl.ds(start, size), :]

    def c_half(n):
        return copy(n, 0, sd.at[lax.rem(n, 2)], pair(n, other, half), partner)

    def c_p1a(n, d):
        return copy(n, 1 + d, s1.at[lax.rem(n, ns1), d, pl.ds(0, 2 * blk), :],
                    one(n, d, other, 2 * blk), first[d])

    def c_p1b(n, d):
        return copy(n, 3 + d, s1.at[lax.rem(n, ns1), d, pl.ds(2 * blk, blk), :],
                    one(n, d, other + 2 * blk, blk), first[d])

    def c_p2a(n, d):
        return copy(n, 5 + d, s2.at[lax.rem(n, ns2), d, pl.ds(0, 2 * sub), :],
                    one(n, d, other + 3 * blk, 2 * sub), second[d])

    def c_p2b(n, d):
        return copy(n, 7 + d, s2.at[lax.rem(n, ns2), d, pl.ds(2 * sub, sub), :],
                    one(n, d, other + 3 * blk + 2 * sub, sub), second[d])

    def c_g2a(n, d):
        ref = pair(n, row(p, q), sub)
        return copy(n, 9 + d, ref, ref, second[d])

    def c_g2b(n, d):
        ref = one(n, d, row(p, q - 1 + 2 * d), sub)
        return copy(n, 11 + d, ref, ref, second[d])

    def c_g1a(n, d):
        ref = pair(n, row(p), blk)
        return copy(n, 13 + d, ref, ref, first[d])

    def c_g1b(n, d):
        ref = one(n, d, row(p - 1 + 2 * d), blk)
        return copy(n, 15 + d, ref, ref, first[d])

    def c_push(n):
        ref = pair(n, mine, half)
        return copy(n, 17, ref, ref, partner)

    def each(f, n, what):
        for d in range(2):
            getattr(f(n, d), what)()

    def got(n, h, start, size):
        return x[2 * n + h, pl.ds(start, size), :].astype(F32)

    def chip(n, h, i):
        at = pl.multiple_of(wrap(i) * blk, blk)
        return acc[lax.rem(n, nacc), h, pl.ds(at, blk), :] + got(n, h, row(i), blk)

    def line(n, h, j):
        at = pl.multiple_of(wrap(j) * sub, sub)
        return r[lax.rem(n, nr), h, pl.ds(at, sub), :]

    def stage1(n):
        c_half(n).wait_recv()
        sl = lax.rem(n, ns1)
        s1[sl, 0, pl.ds(0, blk), :] = chip(n, 1, p + 2).astype(BF16)
        s1[sl, 0, pl.ds(blk, blk), :] = chip(n, 0, p + 1).astype(BF16)
        s1[sl, 1, pl.ds(0, blk), :] = chip(n, 0, p + 2).astype(BF16)
        s1[sl, 1, pl.ds(blk, blk), :] = chip(n, 1, p - 1).astype(BF16)
        each(c_p1a, n, "start")

    def stage2(n):
        each(c_p1a, n, "wait_recv")
        c_half(n).wait_send()
        sl = lax.rem(n, ns1)
        s1[sl, 0, pl.ds(2 * blk, blk), :] = (chip(n, 1, p + 1) + got(n, 0, other, blk)).astype(BF16)
        s1[sl, 1, pl.ds(2 * blk, blk), :] = (chip(n, 0, p - 1) + got(n, 1, other, blk)).astype(BF16)
        each(c_p1b, n, "start")

    def stage3(n):
        each(c_p1b, n, "wait_recv")
        each(c_p1a, n, "wait_send")
        for h in range(2):
            r[lax.rem(n, nr), h] = (chip(n, h, p) + got(n, h, other + blk, blk)
                                    + got(n, 1 - h, other + 2 * blk, blk))
        sl = lax.rem(n, ns2)
        s2[sl, 0, pl.ds(0, sub), :] = line(n, 1, q + 2).astype(BF16)
        s2[sl, 0, pl.ds(sub, sub), :] = line(n, 0, q + 1).astype(BF16)
        s2[sl, 1, pl.ds(0, sub), :] = line(n, 0, q + 2).astype(BF16)
        s2[sl, 1, pl.ds(sub, sub), :] = line(n, 1, q - 1).astype(BF16)
        each(c_p2a, n, "start")

    def stage4(n):
        each(c_p2a, n, "wait_recv")
        each(c_p1b, n, "wait_send")
        sl = lax.rem(n, ns2)
        at = other + 3 * blk
        s2[sl, 0, pl.ds(2 * sub, sub), :] = (line(n, 1, q + 1) + got(n, 0, at, sub)).astype(BF16)
        s2[sl, 1, pl.ds(2 * sub, sub), :] = (line(n, 0, q - 1) + got(n, 1, at, sub)).astype(BF16)
        each(c_p2b, n, "start")

    def stage5(n):
        each(c_p2b, n, "wait_recv")
        each(c_p2a, n, "wait_send")
        at = other + 3 * blk
        for h in range(2):
            total = line(n, h, q) + got(n, h, at + sub, sub) + got(n, 1 - h, at + 2 * sub, sub)
            x[2 * n + h, pl.ds(row(p, q), sub), :] = total.astype(BF16)
        pl.semaphore_signal(credit, 1, device_id={"dp": partner}, device_id_type=MESH)
        each(c_g2a, n, "start")

    def stage6(n):
        each(c_g2a, n, "wait_recv")
        each(c_p2b, n, "wait_send")
        each(c_g2b, n, "start")

    def stage7(n):
        each(c_g2b, n, "wait_recv")
        each(c_g2a, n, "wait_send")
        each(c_g1a, n, "start")

    def stage8(n):
        each(c_g1a, n, "wait_recv")
        each(c_g2b, n, "wait_send")
        each(c_g1b, n, "start")

    def stage9(n):
        each(c_g1b, n, "wait_recv")
        each(c_g1a, n, "wait_send")
        pl.semaphore_wait(credit, 1)
        c_push(n).start()

    def stage10(n):
        c_push(n).wait_recv()
        c_push(n).wait_send()
        each(c_g1b, n, "wait_send")

    stages = (stage1, stage2, stage3, stage4, stage5, stage6, stage7, stage8, stage9, stage10)

    def a_load(m, part):
        cols = (other, mine)[part]
        view = (slice(None), pl.ds(cols, half))
        return pltpu.make_async_copy(a.at[(0, m) + view], abuf.at[(m,) + view], asem.at[m, part])

    def g_load(n, h):
        u = 2 * n + h
        c = pl.multiple_of(lax.rem(u, tiles) * LANES, LANES)
        sl = lax.rem(n, 2)
        return pltpu.make_async_copy(
            g.at[0, u // tiles, :, pl.ds(c, LANES)],
            gbuf.at[sl, :, pl.ds(h * LANES, LANES)], gsem.at[sl, h])

    def product(n, start, put):
        sl = lax.rem(n, 2)

        def dot(m, cols):
            return lax.dot_general(abuf[m, :, pl.ds(start, half)], gbuf[sl, :, cols],
                                   (((0,), (0,)), ((), ())), preferred_element_type=F32)

        @pl.when(n != mixed)
        def _():
            out = dot((2 * n) // tiles, slice(None))
            for h in range(2):
                put(h, out[:, h * LANES:(h + 1) * LANES])

        if mixed >= 0:
            @pl.when(n == mixed)
            def _():
                for h in range(2):
                    put(h, dot((2 * n + h) // tiles, slice(h * LANES, (h + 1) * LANES)))

    def run_stages(step, parity):
        for k in reversed(range(len(stages))):
            if (OFFSETS[k] + 1) % 2 != parity:
                continue
            n = step - (OFFSETS[k] + 1 - parity) // 2

            @pl.when(jnp.logical_and(n >= 0, n < chunks))
            def _(k=k, n=n):
                stages[k](n)

    a_load(0, 0).start()
    for h in range(2):
        g_load(0, h).start()
    a_load(0, 1).start()
    pl.semaphore_wait(bar, 5)

    def step(t, _):
        @pl.when(t < chunks)
        def _():
            @pl.when(t + 1 < chunks)
            def _():
                for h in range(2):
                    g_load(t + 1, h).start()
            for h in range(2):
                g_load(t, h).wait()
            for m in range(mats):
                @pl.when(t == m * tiles // 2)
                def _(m=m):
                    a_load(m, 0).wait()

            def put(h, v):
                sd[lax.rem(t, 2), h] = v.astype(BF16)

            product(t, other, put)
            c_half(t).start()

        run_stages(t, 0)

        @pl.when(t < chunks)
        def _():
            for m in range(mats):
                @pl.when(t == m * tiles // 2)
                def _(m=m):
                    a_load(m, 1).wait()

            def put(h, v):
                acc[lax.rem(t, nacc), h] = v

            product(t, mine, put)
            for m in range(1, mats):
                @pl.when(t == (m - 1) * tiles // 2)
                def _(m=m):
                    for part in range(2):
                        a_load(m, part).start()

        run_stages(t, 1)
        return 0

    lax.fori_loop(0, chunks + (max(OFFSETS) + 1) // 2, step, 0)


def _write_kernel(x, out, sem):
    tiles = x.shape[0] // out.shape[0]

    def moves():
        for u in range(x.shape[0]):
            yield pltpu.make_async_copy(
                x.at[u], out.at[u // tiles, :, pl.ds(u % tiles * LANES, LANES)], sem.at[u])

    for move in moves():
        move.start()
    for move in moves():
        move.wait()


def solution(mesh):
    cores = 2
    side = math.isqrt(mesh.shape["dp"] // cores)

    def body(a, g):
        _, mats, tokens, rows = a.shape
        tiles = g.shape[-1] // LANES
        half = rows // 2
        blk = half // side
        sub = blk // side
        chunks = mats * tiles // 2
        keep = OFFSETS[2] // 2 + 2
        x = pl.pallas_call(
            lambda *refs: _reduce_kernel(side, mats, tiles, *refs),
            out_shape=pltpu.VMEM((mats * tiles, rows, LANES), BF16),
            in_specs=[pl.BlockSpec(memory_space=pl.ANY)] * 2,
            out_specs=pl.BlockSpec(memory_space=pltpu.VMEM),
            scratch_shapes=[
                pltpu.VMEM((mats, tokens, rows), BF16),
                pltpu.VMEM((2, tokens, 2 * LANES), BF16),
                pltpu.VMEM((keep, 2, half, LANES), F32),
                pltpu.VMEM((2, 2, half, LANES), BF16),
                pltpu.VMEM((4, 2, 3 * blk, LANES), BF16),
                pltpu.VMEM((4, 2, blk, LANES), F32),
                pltpu.VMEM((4, 2, 3 * sub, LANES), BF16),
                pltpu.SemaphoreType.DMA((4, 18)),
                pltpu.SemaphoreType.DMA((chunks, 18)),
                pltpu.SemaphoreType.DMA((mats, 2)),
                pltpu.SemaphoreType.DMA((2, 2)),
                pltpu.SemaphoreType.REGULAR,
            ],
            compiler_params=pltpu.CompilerParams(
                collective_id=0, has_side_effects=True, vmem_limit_bytes=39 * 2**20),
            name="reduce",
        )(a, g)
        return pl.pallas_call(
            _write_kernel,
            out_shape=jax.ShapeDtypeStruct((mats, rows, tiles * LANES), BF16),
            in_specs=[pl.BlockSpec(memory_space=pltpu.VMEM)],
            out_specs=pl.BlockSpec(memory_space=pl.ANY),
            scratch_shapes=[pltpu.SemaphoreType.DMA((mats * tiles,))],
            compiler_params=pltpu.CompilerParams(vmem_limit_bytes=2**20),
            name="write",
        )(x)

    spec = P(("rep", "dp"))
    return jax.shard_map(body, mesh=mesh, in_specs=(spec, spec), out_specs=P("rep"), check_vma=False)
```

time: 478 us -> 233 us (0.49)
  blocking collectives: 350 us -> 0 us
  Pallas kernels: 0 us -> 233 us
  matrix products: 128 us -> 0 us
    dot_general x1 -> x0, blocking collectives: 350 us -> none  [step(): jnp.einsum('rsntd,rsntf->rndf', a, g, preferred_element_type=jnp.float32)]
    pallas_call x0 -> x2, Pallas kernels: none -> 233 us  [the longest x1 223 us: body(): pl.pallas_call(lambda *refs: _reduce_kernel(side, mats, tiles, *refs), ou...]
    dot_general x1 -> x0, matrix products: 128 us -> none  [step(): jnp.einsum('rsntd,rsntf->rndf', a, g, preferred_element_type=jnp.float32)]
where the time goes in v1:
time: 233 us
  Pallas kernels  233 us (100%)
    pallas_call x1, Pallas kernels, body(): pl.pallas_call(lambda *refs: _reduce_kernel(side, mats, tiles, *refs), ou...  223 us
    pallas_call x1, Pallas kernels, body(): pl.pallas_call(_write_kernel, out_shape=jax.ShapeDtypeStruct((mats, rows,...  9.12 us

profile of v1, /device:TPU:97, one launch (start us, length us, event | category | flops | bytes accessed | tf_op | source)
XLA Modules:
  0.0 232.6 jit_solution(7609613931852555772)
XLA Ops:
  0.0 223.4 %reduce.1.x = bf16[66,1536,128]{2,1,0:T(8,128)(2,1)S(1)} custom-call(bf16[1,2,4096,1536]{3,2,1,0:T(8,128)(2,1)} %refs_0_.1, bf16[1,2,4096,4224]{3,2,1,0:T(8,128)(2,1)} %refs_1_.1), custom_call_target="tpu_custom_call" | custom-call | tf_op jit(solution)/shard_map/reduce/pallas_call | solution.py:315
  223.5 9.1 %write.1 = bf16[2,1536,4224]{2,1,0:T(8,128)(2,1)} custom-call(bf16[66,1536,128]{2,1,0:T(8,128)(2,1)S(1)} %reduce.1.x), custom_call_target="tpu_custom_call" | custom-call | tf_op jit(solution)/shard_map/write/pallas_call | solution.py:338

commit v2 on v1

v2 whole, which is shorter than its diff:
```python
import math

import jax
import jax.numpy as jnp
from jax import lax
from jax.experimental import pallas as pl
from jax.experimental.pallas import tpu as pltpu
from jax.sharding import PartitionSpec as P

MESH = pl.DeviceIdType.MESH
HALF, P1A, P1B, P2A, P2B, G2A, G2B, G1A, G1B, PUSH = range(10)
SENT = (0, 1, 1, 2, 2, 3, 3, 3, 3, 3)
LANES = 128
F32 = jnp.float32
BF16 = jnp.bfloat16
OFFSETS = (1, 3, 4, 5, 6, 7, 8, 10, 12, 13)
ORDER = (5, 6, 4, 3, 2, 1, 7, 8, 9, 10)


def _reduce_kernel(side, mats, tiles, a, g, x, abuf, gbuf, acc, sd, s1, r, s2,
                   ssem, rsem, asem, gsem, credit):
    rows = x.shape[1]
    half = rows // 2
    blk = half // side
    sub = blk // side
    chunks = mats * tiles // 2
    mixed = tiles // 2 if tiles % 2 else -1
    nacc = acc.shape[0]

    def slot(n):
        return n & 7

    def acc_slot(n):
        return n - nacc * (n * (1024 // nacc + 1) // 1024)

    me = lax.axis_index("dp")
    core = lax.rem(me, 2)
    cy = lax.rem(me // 2, side)
    cx = me // (2 * side)
    p = jnp.where(core == 0, cx, cy)
    q = jnp.where(core == 0, cy, cx)

    def dev(i, j):
        return jnp.where(core == 0, (i * side + j) * 2, (j * side + i) * 2 + 1)

    def wrap(v):
        return lax.rem(v + 2 * side, side)

    first = (dev(wrap(p + 1), q), dev(wrap(p - 1), q))
    second = (dev(p, wrap(q + 1)), dev(p, wrap(q - 1)))
    partner = me + 1 - 2 * core
    mine = pl.multiple_of(core * half, half)
    other = pl.multiple_of((1 - core) * half, half)

    bar = pltpu.get_barrier_semaphore()
    for d in (*first, *second, partner):
        pl.semaphore_signal(bar, 1, device_id={"dp": d}, device_id_type=MESH)

    def copy(n, kind, src, dst, to):
        return pltpu.make_async_remote_copy(
            src_ref=src, dst_ref=dst, send_sem=ssem.at[slot(n), SENT[kind]],
            recv_sem=rsem.at[n, kind], device_id={"dp": to}, device_id_type=MESH)

    def landed(n, kind, size):
        ref = pair(n, 0, size)
        pltpu.make_async_copy(ref, ref, rsem.at[n, kind]).wait()

    def left(n, group, size):
        ref = pair(n, 0, size)
        pltpu.make_async_copy(ref, ref, ssem.at[slot(n), group]).wait()

    def row(i, j=0):
        return pl.multiple_of(mine + wrap(i) * blk + wrap(j) * sub, sub)

    first_at = {i: pl.multiple_of(wrap(p + i) * blk, blk) for i in (-1, 0, 1, 2)}
    second_at = {j: pl.multiple_of(wrap(q + j) * sub, sub) for j in (-1, 0, 1, 2)}
    home = {(i, j): row(p + i, q + j) for i, j in ((0, 0), (0, -1), (0, 1))}
    row_at = {i: row(p + i) for i in (-1, 0, 1, 2)}

    def pair(n, start, size):
        return x.at[pl.ds(2 * n, 2), pl.ds(start, size), :]

    def one(n, h, start, size):
        return x.at[2 * n + h, pl.ds(start, size), :]

    def c_half(n):
        return copy(n, HALF, sd.at[(n & 1)], pair(n, other, half), partner)

    def c_p1a(n, d):
        return copy(n, P1A, s1.at[n & 3, d, pl.ds(0, 2 * blk), :],
                    one(n, d, other, 2 * blk), first[d])

    def c_p1b(n, d):
        return copy(n, P1B, s1.at[n & 3, d, pl.ds(2 * blk, blk), :],
                    one(n, d, other + 2 * blk, blk), first[d])

    def c_p2a(n, d):
        return copy(n, P2A, s2.at[slot(n), d, pl.ds(0, 2 * sub), :],
                    one(n, d, other + 3 * blk, 2 * sub), second[d])

    def c_p2b(n, d):
        return copy(n, P2B, s2.at[slot(n), d, pl.ds(2 * sub, sub), :],
                    one(n, d, other + 3 * blk + 2 * sub, sub), second[d])

    def c_g2a(n, d):
        ref = pair(n, home[0, 0], sub)
        return copy(n, G2A, ref, ref, second[d])

    def c_g2b(n, d):
        ref = one(n, d, home[0, 2 * d - 1], sub)
        return copy(n, G2B, ref, ref, second[d])

    def c_g1a(n, d):
        ref = pair(n, row_at[0], blk)
        return copy(n, G1A, ref, ref, first[d])

    def c_g1b(n, d):
        ref = one(n, d, row_at[2 * d - 1], blk)
        return copy(n, G1B, ref, ref, first[d])

    def c_push(n):
        ref = pair(n, mine, half)
        return copy(n, PUSH, ref, ref, partner)

    def each(f, n, what):
        for d in range(2):
            getattr(f(n, d), what)()

    def got(n, h, start, size):
        return x[2 * n + h, pl.ds(start, size), :].astype(F32)

    def chip(n, h, i):
        return acc[acc_slot(n), h, pl.ds(first_at[i], blk), :] + got(n, h, row_at[i], blk)

    def line(n, h, j):
        return r[n & 3, h, pl.ds(second_at[j], sub), :]

    def stage1(n):
        c_half(n).wait_recv()
        c_half(n).wait_send()
        sl = n & 3
        s1[sl, 0, pl.ds(0, blk), :] = chip(n, 1, 2).astype(BF16)
        s1[sl, 0, pl.ds(blk, blk), :] = chip(n, 0, 1).astype(BF16)
        s1[sl, 1, pl.ds(0, blk), :] = chip(n, 0, 2).astype(BF16)
        s1[sl, 1, pl.ds(blk, blk), :] = chip(n, 1, -1).astype(BF16)
        each(c_p1a, n, "start")

    def stage2(n):
        landed(n, P1A, 2 * blk)
        sl = n & 3
        s1[sl, 0, pl.ds(2 * blk, blk), :] = (chip(n, 1, 1) + got(n, 0, other, blk)).astype(BF16)
        s1[sl, 1, pl.ds(2 * blk, blk), :] = (chip(n, 0, -1) + got(n, 1, other, blk)).astype(BF16)
        each(c_p1b, n, "start")

    def stage3(n):
        landed(n, P1B, blk)
        for h in range(2):
            r[(n & 3), h] = (chip(n, h, 0) + got(n, h, other + blk, blk)
                                    + got(n, 1 - h, other + 2 * blk, blk))
        sl = slot(n)
        s2[sl, 0, pl.ds(0, sub), :] = line(n, 1, 2).astype(BF16)
        s2[sl, 0, pl.ds(sub, sub), :] = line(n, 0, 1).astype(BF16)
        s2[sl, 1, pl.ds(0, sub), :] = line(n, 0, 2).astype(BF16)
        s2[sl, 1, pl.ds(sub, sub), :] = line(n, 1, -1).astype(BF16)
        each(c_p2a, n, "start")

    def stage4(n):
        landed(n, P2A, 2 * sub)
        left(n, 1, 3 * blk)
        sl = slot(n)
        at = other + 3 * blk
        s2[sl, 0, pl.ds(2 * sub, sub), :] = (line(n, 1, 1) + got(n, 0, at, sub)).astype(BF16)
        s2[sl, 1, pl.ds(2 * sub, sub), :] = (line(n, 0, -1) + got(n, 1, at, sub)).astype(BF16)
        each(c_p2b, n, "start")

    def stage5(n):
        landed(n, P2B, sub)
        at = other + 3 * blk
        for h in range(2):
            total = line(n, h, 0) + got(n, h, at + sub, sub) + got(n, 1 - h, at + 2 * sub, sub)
            x[2 * n + h, pl.ds(home[0, 0], sub), :] = total.astype(BF16)
        pl.semaphore_signal(credit, 1, device_id={"dp": partner}, device_id_type=MESH)
        each(c_g2a, n, "start")

    def stage6(n):
        landed(n, G2A, 2 * sub)
        left(n, 2, 3 * sub)
        each(c_g2b, n, "start")

    def stage7(n):
        landed(n, G2B, sub)
        each(c_g1a, n, "start")

    def stage8(n):
        landed(n, G1A, 2 * blk)
        each(c_g1b, n, "start")

    def stage9(n):
        landed(n, G1B, blk)
        pl.semaphore_wait(credit, 1)
        c_push(n).start()

    def stage10(n):
        c_push(n).wait_recv()
        left(n, 3, half + 3 * blk + 3 * sub)

    stages = (stage1, stage2, stage3, stage4, stage5, stage6, stage7, stage8, stage9, stage10)

    def a_load(m, part):
        cols = (other, mine)[part]
        view = (slice(None), pl.ds(cols, half))
        return pltpu.make_async_copy(a.at[(0, m) + view], abuf.at[(m,) + view], asem.at[m, part])

    def g_load(n, h):
        u = 2 * n + h
        c = pl.multiple_of(lax.rem(u, tiles) * LANES, LANES)
        sl = (n & 1)
        return pltpu.make_async_copy(
            g.at[0, u // tiles, :, pl.ds(c, LANES)],
            gbuf.at[sl, :, pl.ds(h * LANES, LANES)], gsem.at[sl, h])

    def product(n, same):
        sl = (n & 1)

        def dot(start, h, cols):
            return lax.dot_general(abuf[(2 * n + h) // tiles, :, pl.ds(start, half)], gbuf[sl, :, cols],
                                   (((0,), (0,)), ((), ())), preferred_element_type=F32)

        def halves(start):
            if same:
                both = dot(start, 0, slice(None))
                return [both[:, h * LANES:(h + 1) * LANES] for h in range(2)]
            return [lax.dot_general(
                gbuf[sl, :, h * LANES:(h + 1) * LANES], abuf[(2 * n + h) // tiles, :, pl.ds(start, half)],
                (((0,), (0,)), ((), ())), preferred_element_type=F32).T for h in range(2)]

        for h, v in enumerate(halves(other)):
            sd[sl, h] = v.astype(BF16)
        for h, v in enumerate(halves(mine)):
            acc[acc_slot(n), h] = v
        c_half(n).start()

    def run_stages(t):
        for k in ORDER:
            n = t - OFFSETS[k - 1]

            @pl.when(jnp.logical_and(n >= 0, n < chunks))
            def _(k=k, n=n):
                stages[k - 1](n)

    a_load(0, 0).start()
    for h in range(2):
        g_load(0, h).start()
    a_load(0, 1).start()
    pl.semaphore_wait(bar, 5)

    def step(t, _):
        @pl.when(t < chunks)
        def _():
            @pl.when(t + 1 < chunks)
            def _():
                for h in range(2):
                    g_load(t + 1, h).start()
            for m in range(mats):
                @pl.when(t == m * tiles // 2)
                def _(m=m):
                    for part in range(2):
                        a_load(m, part).wait()
            for h in range(2):
                g_load(t, h).wait()
            for m in range(1, mats):
                @pl.when(t == (m - 1) * tiles // 2 + 1)
                def _(m=m):
                    for part in range(2):
                        a_load(m, part).start()

        @pl.when(jnp.logical_and(t < chunks, t != mixed))
        def _():
            product(t, True)

        if mixed >= 0:
            @pl.when(t == mixed)
            def _():
                product(t, False)

        run_stages(t)
        return 0

    lax.fori_loop(0, chunks + max(OFFSETS), step, 0)


def _write_kernel(x, out, sem):
    tiles = x.shape[0] // out.shape[0]

    def moves():
        for u in range(x.shape[0]):
            yield pltpu.make_async_copy(
                x.at[u], out.at[u // tiles, :, pl.ds(u % tiles * LANES, LANES)], sem.at[u])

    for move in moves():
        move.start()
    for move in moves():
        move.wait()


def solution(mesh):
    cores = 2
    side = math.isqrt(mesh.shape["dp"] // cores)

    def body(a, g):
        _, mats, tokens, rows = a.shape
        tiles = g.shape[-1] // LANES
        half = rows // 2
        blk = half // side
        sub = blk // side
        chunks = mats * tiles // 2
        keep = OFFSETS[2] + 1
        x = pl.pallas_call(
            lambda *refs: _reduce_kernel(side, mats, tiles, *refs),
            out_shape=pltpu.VMEM((mats * tiles, rows, LANES), BF16),
            in_specs=[pl.BlockSpec(memory_space=pl.ANY)] * 2,
            out_specs=pl.BlockSpec(memory_space=pltpu.VMEM),
            scratch_shapes=[
                pltpu.VMEM((mats, tokens, rows), BF16),
                pltpu.VMEM((2, tokens, 2 * LANES), BF16),
                pltpu.VMEM((keep, 2, half, LANES), F32),
                pltpu.VMEM((2, 2, half, LANES), BF16),
                pltpu.VMEM((4, 2, 3 * blk, LANES), BF16),
                pltpu.VMEM((4, 2, blk, LANES), F32),
                pltpu.VMEM((8, 2, 3 * sub, LANES), BF16),
                pltpu.SemaphoreType.DMA((8, 4)),
                pltpu.SemaphoreType.DMA((chunks, 10)),
                pltpu.SemaphoreType.DMA((mats, 2)),
                pltpu.SemaphoreType.DMA((2, 2)),
                pltpu.SemaphoreType.REGULAR,
            ],
            compiler_params=pltpu.CompilerParams(
                collective_id=0, has_side_effects=True, vmem_limit_bytes=39 * 2**20),
            name="reduce",
        )(a, g)
        return pl.pallas_call(
            _write_kernel,
            out_shape=jax.ShapeDtypeStruct((mats, rows, tiles * LANES), BF16),
            in_specs=[pl.BlockSpec(memory_space=pltpu.VMEM)],
            out_specs=pl.BlockSpec(memory_space=pl.ANY),
            scratch_shapes=[pltpu.SemaphoreType.DMA((mats * tiles,))],
            compiler_params=pltpu.CompilerParams(vmem_limit_bytes=2**20),
            name="write",
        )(x)

    spec = P(("rep", "dp"))
    return jax.shard_map(body, mesh=mesh, in_specs=(spec, spec), out_specs=P("rep"), check_vma=False)
```

time: 233 us -> 199 us (0.85)
  Pallas kernels: 233 us -> 199 us
    pallas_call x1, Pallas kernels: 223 us -> 190 us  [body(): pl.pallas_call(lambda *refs: _reduce_kernel(side, mats, tiles, *refs), ou...]
where the time goes in v2:
time: 199 us
  Pallas kernels  199 us (100%)
    pallas_call x1, Pallas kernels, body(): pl.pallas_call(lambda *refs: _reduce_kernel(side, mats, tiles, *refs), ou...  190 us
    pallas_call x1, Pallas kernels, body(): pl.pallas_call(_write_kernel, out_shape=jax.ShapeDtypeStruct((mats, rows,...  9.12 us

profile of v2, /device:TPU:97, one launch (start us, length us, event | category | flops | bytes accessed | tf_op | source)
XLA Modules:
  0.0 198.7 jit_solution(5420560136229706163)
XLA Ops:
  0.0 189.5 %reduce.1.x = bf16[66,1536,128]{2,1,0:T(8,128)(2,1)S(1)} custom-call(bf16[1,2,4096,1536]{3,2,1,0:T(8,128)(2,1)} %refs_0_.1, bf16[1,2,4096,4224]{3,2,1,0:T(8,128)(2,1)} %refs_1_.1), custom_call_target="tpu_custom_call" | custom-call | tf_op jit(solution)/shard_map/reduce/pallas_call | solution.py:318
  189.5 9.1 %write.1 = bf16[2,1536,4224]{2,1,0:T(8,128)(2,1)} custom-call(bf16[66,1536,128]{2,1,0:T(8,128)(2,1)S(1)} %reduce.1.x), custom_call_target="tpu_custom_call" | custom-call | tf_op jit(solution)/shard_map/write/pallas_call | solution.py:341

commit v3 on v2

--- a/solution.py
+++ b/solution.py
@@ -154,6 +154,7 @@
 
     def stage3(n):
         landed(n, P1B, blk)
+        left(n, 1, 3 * blk)
         for h in range(2):
             r[(n & 3), h] = (chip(n, h, 0) + got(n, h, other + blk, blk)
                                     + got(n, 1 - h, other + 2 * blk, blk))
@@ -166,7 +167,6 @@
 
     def stage4(n):
         landed(n, P2A, 2 * sub)
-        left(n, 1, 3 * blk)
         sl = slot(n)
         at = other + 3 * blk
         s2[sl, 0, pl.ds(2 * sub, sub), :] = (line(n, 1, 1) + got(n, 0, at, sub)).astype(BF16)
@@ -244,7 +244,7 @@
         for k in ORDER:
             n = t - OFFSETS[k - 1]
 
-            @pl.when(jnp.logical_and(n >= 0, n < chunks))
+            @pl.when(n >= 0)
             def _(k=k, n=n):
                 stages[k - 1](n)
 
@@ -255,26 +255,24 @@
     pl.semaphore_wait(bar, 5)
 
     def step(t, _):
-        @pl.when(t < chunks)
+        @pl.when(t + 1 < chunks)
         def _():
-            @pl.when(t + 1 < chunks)
-            def _():
-                for h in range(2):
-                    g_load(t + 1, h).start()
-            for m in range(mats):
-                @pl.when(t == m * tiles // 2)
-                def _(m=m):
-                    for part in range(2):
-                        a_load(m, part).wait()
             for h in range(2):
-                g_load(t, h).wait()
-            for m in range(1, mats):
-                @pl.when(t == (m - 1) * tiles // 2 + 1)
-                def _(m=m):
-                    for part in range(2):
-                        a_load(m, part).start()
-
-        @pl.when(jnp.logical_and(t < chunks, t != mixed))
+                g_load(t + 1, h).start()
+        for m in range(mats):
+            @pl.when(t == m * tiles // 2)
+            def _(m=m):
+                for part in range(2):
+                    a_load(m, part).wait()
+        for h in range(2):
+            g_load(t, h).wait()
+        for m in range(1, mats):
+            @pl.when(t == (m - 1) * tiles // 2 + 1)
+            def _(m=m):
+                for part in range(2):
+                    a_load(m, part).start()
+
+        @pl.when(t != mixed)
         def _():
             product(t, True)
 
@@ -286,7 +284,13 @@
         run_stages(t)
         return 0
 
-    lax.fori_loop(0, chunks + max(OFFSETS), step, 0)
+    lax.fori_loop(0, chunks, step, 0)
+
+    todo = {n: sum(n + o < chunks for o in OFFSETS) for n in range(chunks)}
+    while any(k < len(stages) for k in todo.values()):
+        for n in sorted((n for n in todo if todo[n] < len(stages)), key=lambda n: ORDER.index(todo[n] + 1)):
+            stages[todo[n]](n)
+            todo[n] += 1
 
 
 def _write_kernel(x, out, sem):

time: 199 us -> 196 us (0.985)
  Pallas kernels: 199 us -> 196 us
    pallas_call x1, Pallas kernels: 190 us -> 187 us  [body(): pl.pallas_call(lambda *refs: _reduce_kernel(side, mats, tiles, *refs), ou...]
where the time goes in v3:
time: 196 us
  Pallas kernels  196 us (100%)
    pallas_call x1, Pallas kernels, body(): pl.pallas_call(lambda *refs: _reduce_kernel(side, mats, tiles, *refs), ou...  187 us
    pallas_call x1, Pallas kernels, body(): pl.pallas_call(_write_kernel, out_shape=jax.ShapeDtypeStruct((mats, rows,...  9.12 us

profile of v3, /device:TPU:97, one launch (start us, length us, event | category | flops | bytes accessed | tf_op | source)
XLA Modules:
  0.0 195.7 jit_solution(8151069236309901079)
XLA Ops:
  0.0 186.6 %reduce.1.x = bf16[66,1536,128]{2,1,0:T(8,128)(2,1)S(1)} custom-call(bf16[1,2,4096,1536]{3,2,1,0:T(8,128)(2,1)} %refs_0_.1, bf16[1,2,4096,4224]{3,2,1,0:T(8,128)(2,1)} %refs_1_.1), custom_call_target="tpu_custom_call" | custom-call | tf_op jit(solution)/shard_map/reduce/pallas_call | solution.py:322
  186.6 9.1 %write.1 = bf16[2,1536,4224]{2,1,0:T(8,128)(2,1)} custom-call(bf16[66,1536,128]{2,1,0:T(8,128)(2,1)S(1)} %reduce.1.x), custom_call_target="tpu_custom_call" | custom-call | tf_op jit(solution)/shard_map/write/pallas_call | solution.py:345
